TPU v7x, 32 devices: a whole 2x2x4 slice. The times are simulated.
32 devices in a mesh: replica: 4 (over y, core), shard: 8 (over z, x).
Axes of the slice: x: 2, y: 2, z: 4, core: 2. Of those that a mesh axis runs over, the one named last changes fastest.
Arguments:
- anchor: float32 [384, 8192], P('shard'), may hold values from -6 to 6
- replica_rows: bfloat16 [4, 384, 8192], P('replica', 'shard'), may hold values from -6 to 6
- outer_velocity: float32 [384, 8192], P('shard', 'replica'), may hold values from -6 to 6
- features: bfloat16 [4, 384, 256], P('replica', 'shard'), may hold values from -6 to 6
- cotangent: bfloat16 [4, 256, 1024], P('replica', 'shard'), may hold values from -0.375 to 0.375
- inner_weight: float32 [4, 384, 1024], P('replica', 'shard'), may hold values from -6 to 6
- first_moment: float32 [4, 384, 1024], P('replica', 'shard'), may hold values from -6 to 6
- second_moment: float32 [4, 384, 1024], P('replica', 'shard'), may hold values from 0.5 to 2
Outputs:
- new_anchor: float32 [384, 8192], P('shard')
- merged_rows: bfloat16 [4, 384, 8192], P('replica', 'shard')
- new_velocity: float32 [384, 8192], P('shard', 'replica')
- new_weight: float32 [4, 384, 1024], P('replica', 'shard')
- new_first: float32 [4, 384, 1024], P('replica', 'shard')
- new_second: float32 [4, 384, 1024], P('replica', 'shard')
All inputs are finite; a program needn't handle non-finite values.
Results may differ from a plain program's by a relative error of at most 0.0035.
Values may be sent and summed in bfloat16 or wider, within the bound.
A program may use at most 64 MiB of HBM per device.

v0:
```python
import functools

import jax
import jax.numpy as jnp
from jax import lax
from jax.experimental import pallas as pl
from jax.experimental.pallas import tpu as pltpu
from jax.sharding import PartitionSpec as P

momentum_keep = 0.9
outer_rate = 0.7
blend_keep = 0.5
inner_rate = 0.01
decay_first = 0.9
decay_second = 0.95
weight_decay = 0.1
epsilon = 1e-08
first_fix = 1.0 - 0.9**10
second_fix = 1.0 - 0.95**10

MESH = pl.DeviceIdType.MESH
SPLIT = 4
PARTS = 4


def kernel(R, S, anchor_h, rows_h, vel_h, feat_h, cot_h, w_h, m_h, s_h,
           na_o, mg_o, nv_o, nw_o, nm_o, ns_o,
           anchor, rows, vel, feat, cot, w, m, s, sib_rows, msg,
           in_sem, sib_send, sib_recv, y_send, fwd_send, msg_recv,
           cot_own_send, cot_z_send, cot_x_send, cot_recv):
    C = R // 2
    H = SPLIT
    me, at = lax.axis_index("replica"), lax.axis_index("shard")
    y, c = me // 2, me % 2
    sib = me + 1 - 2 * c
    partner = at + 1 - 2 * (at % 2)
    pos, length = at // 2, S // 2
    W = vel.shape[1]
    piece = W // H
    depth = cot_h.shape[1]
    part_width = cot_h.shape[2] // PARTS

    def columns(q, h):
        return pl.ds(pl.multiple_of(q * W + h * piece, 128), piece)

    def quarter(q):
        return pl.ds(pl.multiple_of(q * W, 128), W)

    def tokens(k):
        return pl.ds(pl.multiple_of(k * depth, depth), depth)

    def block_part(k, u):
        return cot.at[tokens(k), pl.ds(u * part_width, part_width)]

    barrier = pltpu.get_barrier_semaphore()
    pl.semaphore_signal(barrier, inc=1, device_id={"replica": sib}, device_id_type=MESH)
    for t in range(1, C):
        pl.semaphore_signal(barrier, inc=1, device_id={"replica": lax.rem(me + 2 * t, R)}, device_id_type=MESH)
    pl.semaphore_signal(barrier, inc=1, device_id={"shard": partner}, device_id_type=MESH)

    @pl.when(pos > 0)
    def _():
        pl.semaphore_signal(barrier, inc=1, device_id={"shard": at - 2}, device_id_type=MESH)

    @pl.when(pos < length - 1)
    def _():
        pl.semaphore_signal(barrier, inc=1, device_id={"shard": at + 2}, device_id_type=MESH)

    loads = {}
    slot = 0

    def load(name, src, dst):
        nonlocal slot
        copy = pltpu.make_async_copy(src, dst, in_sem.at[slot])
        copy.start()
        slot += 1
        loads[name] = copy

    load("cot", cot_h.at[0], cot.at[tokens(at)])
    for j in range(C):
        q = 2 * j + 1 - c
        load(("out", j), rows_h.at[0, :, quarter(q)], rows.at[:, quarter(q)])
    for j in range(C):
        q = 2 * j + c
        load(("keep", j), rows_h.at[0, :, quarter(q)], rows.at[:, quarter(q)])
    load("anchor", anchor_h, anchor)
    load("vel", vel_h, vel)
    load("feat", feat_h.at[0], feat)
    load("w", w_h.at[0], w)
    load("m", m_h.at[0], m)
    load("s", s_h.at[0], s)

    count = 2 + (C - 1) + (pos > 0).astype(jnp.int32) + (pos < length - 1).astype(jnp.int32)
    pl.semaphore_wait(barrier, count)

    def sib_copy(j, h):
        return pltpu.make_async_remote_copy(
            src_ref=rows.at[:, columns(2 * j + 1 - c, h)], dst_ref=sib_rows.at[j, h],
            send_sem=sib_send.at[j, h], recv_sem=sib_recv.at[j, h],
            device_id={"replica": sib}, device_id_type=MESH)

    def cot_copy(k, u, send_sem, target):
        return pltpu.make_async_remote_copy(
            src_ref=block_part(k, u), dst_ref=block_part(k, u),
            send_sem=send_sem.at[u], recv_sem=cot_recv.at[k, u],
            device_id={"shard": target}, device_id_type=MESH)

    for j in range(C):
        loads[("out", j)].wait()
        for h in range(H):
            sib_copy(j, h).start()

    loads["cot"].wait()
    cot_right = [cot_copy(at, u, cot_own_send.at[0], at + 2) for u in range(PARTS)]
    cot_left = [cot_copy(at, u, cot_own_send.at[1], at - 2) for u in range(PARTS)]
    cot_across = [cot_copy(at, u, cot_own_send.at[2], partner) for u in range(PARTS)]

    @pl.when(pos < length - 1)
    def _():
        for copy in cot_right:
            copy.start()

    @pl.when(pos > 0)
    def _():
        for copy in cot_left:
            copy.start()

    for copy in cot_across:
        copy.start()

    def y_copy(t, j, h):
        return pltpu.make_async_remote_copy(
            src_ref=msg.at[c, y, j, h], dst_ref=msg.at[c, y, j, h],
            send_sem=y_send.at[t - 1, j, h], recv_sem=msg_recv.at[c, y, j, h],
            device_id={"replica": lax.rem(me + 2 * t, R)}, device_id_type=MESH)

    def to_sib(src, j, h):
        return pltpu.make_async_remote_copy(
            src_ref=msg.at[c, src, j, h], dst_ref=msg.at[c, src, j, h],
            send_sem=fwd_send.at[src, j, h], recv_sem=msg_recv.at[c, src, j, h],
            device_id={"replica": sib}, device_id_type=MESH)

    def arrival(p, src, j, h):
        return pltpu.make_async_remote_copy(
            src_ref=msg.at[p, src, j, h], dst_ref=msg.at[p, src, j, h],
            send_sem=fwd_send.at[src, j, h], recv_sem=msg_recv.at[p, src, j, h],
            device_id={"replica": sib}, device_id_type=MESH)

    c1 = outer_rate * (1.0 + momentum_keep)
    c2 = outer_rate * momentum_keep * momentum_keep
    share = c1 / R
    for j in range(C):
        loads[("keep", j)].wait()
        if j == 0:
            loads["anchor"].wait()
            loads["vel"].wait()
        mine = y == j
        of_anchor = jnp.where(mine, 0.0, 2.0)
        of_rows = jnp.where(mine, share, -1.0)
        of_vel = jnp.where(mine, -c2, 0.0)
        for h in range(H):
            sib_copy(j, h).wait_recv()
            cols = columns(2 * j + c, h)
            both = rows[:, cols].astype(jnp.float32) + sib_rows[j, h].astype(jnp.float32)
            value = of_anchor * anchor[:, cols] + of_rows * both
            value = value + of_vel * vel[:, h * piece:(h + 1) * piece]
            msg[c, y, j, h] = value.astype(jnp.bfloat16)
            for t in range(1, C):
                y_copy(t, j, h).start()
            to_sib(y, j, h).start()

    def finish(p, j, h):
        cols = columns(2 * j + p, h)
        others = msg[p, (j + 1) % C, j, h].astype(jnp.float32)
        for t in range(2, C):
            others = others + msg[p, (j + t) % C, j, h].astype(jnp.float32)
        own = msg[p, j, j, h].astype(jnp.float32)
        new_anchor = (1.0 - 2.0 * share) * anchor[:, cols] + own - share * others
        na_o[:, cols] = new_anchor
        mg_o[0, :, cols] = (
            blend_keep * rows[:, cols].astype(jnp.float32) + (1.0 - blend_keep) * new_anchor
        ).astype(jnp.bfloat16)

    def finish_velocity(j, h):
        @pl.when(y == j)
        def _():
            cols = columns(2 * j + c, h)
            part = slice(h * piece, (h + 1) * piece)
            total = 2.0 * anchor[:, cols] - (
                rows[:, cols].astype(jnp.float32) + sib_rows[j, h].astype(jnp.float32))
            for t in range(1, C):
                total = total + msg[c, (j + t) % C, j, h].astype(jnp.float32)
            nv_o[:, part] = momentum_keep * vel[:, part] + total / R

    def finish_sib(j, h):
        for src in range(C):
            arrival(1 - c, src, j, h).wait_recv()
        finish(1 - c, j, h)

    def cot_step(t, u):
        @pl.when(pos >= t)
        def _():
            k = at - 2 * t
            cot_copy(k, u, cot_x_send.at[0], partner).wait_recv()

            @pl.when(pos < length - 1)
            def _():
                cot_copy(k, u, cot_z_send.at[0, t - 1], at + 2).start()

            cot_copy(k, u, cot_x_send.at[k // 2], partner).start()

        @pl.when(pos + t < length)
        def _():
            k = at + 2 * t
            cot_copy(k, u, cot_x_send.at[0], partner).wait_recv()

            @pl.when(pos > 0)
            def _():
                cot_copy(k, u, cot_z_send.at[1, t - 1], at - 2).start()

            cot_copy(k, u, cot_x_send.at[k // 2], partner).start()

    pieces = [(j, h) for j in range(C) for h in range(H)]
    todo = [(t, u) for t in range(1, length) for u in range(PARTS)]
    before = None
    for i, (j, h) in enumerate(pieces):
        while todo and 3 * (todo[0][0] - 1) + todo[0][1] // 2 <= i + 2:
            cot_step(*todo.pop(0))
        for t in range(1, C):
            src = lax.rem(y + t, C)
            arrival(c, src, j, h).wait_recv()
            to_sib(src, j, h).start()
        finish(c, j, h)
        finish_velocity(j, h)
        if before is not None:
            finish_sib(*before)
        before = (j, h)
    for step in todo:
        cot_step(*step)

    for k in range(length):
        for u in range(PARTS):
            cot_copy(2 * k + 1 - at % 2, u, cot_x_send.at[0], partner).wait_recv()
    for name in ("feat", "w", "m", "s"):
        loads[name].wait()
    tile = min(256, w.shape[1])
    for n in range(w.shape[1] // tile):
        part = slice(n * tile, (n + 1) * tile)
        gradient = jnp.dot(feat[...], cot[:, part], preferred_element_type=jnp.float32)
        new_first = decay_first * m[:, part] + (1.0 - decay_first) * gradient
        new_second = decay_second * s[:, part] + (1.0 - decay_second) * gradient * gradient
        stepped = new_first / first_fix / (jnp.sqrt(new_second / second_fix) + epsilon)
        weight = w[:, part]
        nw_o[0, :, part] = weight - inner_rate * (stepped + weight_decay * weight)
        nm_o[0, :, part] = new_first
        ns_o[0, :, part] = new_second

    finish_sib(*before)

    for j, h in pieces:
        sib_copy(j, h).wait_send()
        for t in range(1, C):
            y_copy(t, j, h).wait_send()
        for src in range(C):
            to_sib(src, j, h).wait_send()
    for copy in cot_across:
        copy.wait_send()

    @pl.when(pos < length - 1)
    def _():
        for copy in cot_right:
            copy.wait_send()

    @pl.when(pos > 0)
    def _():
        for copy in cot_left:
            copy.wait_send()

    for t, u in [(t, u) for t in range(1, length) for u in range(PARTS)]:
        @pl.when(pos >= t)
        def _():
            k = at - 2 * t

            @pl.when(pos < length - 1)
            def _():
                cot_copy(k, u, cot_z_send.at[0, t - 1], at + 2).wait_send()

            cot_copy(k, u, cot_x_send.at[k // 2], partner).wait_send()

        @pl.when(pos + t < length)
        def _():
            k = at + 2 * t

            @pl.when(pos > 0)
            def _():
                cot_copy(k, u, cot_z_send.at[1, t - 1], at - 2).wait_send()

            cot_copy(k, u, cot_x_send.at[k // 2], partner).wait_send()


def store_kernel(*refs):
    sems = refs[-1]
    count = (len(refs) - 1) // 2
    copies = []
    for source, target in zip(refs[:count], refs[count:-1]):
        rows = source.shape[-2]
        cuts = 3 if rows % 48 == 0 else 1
        for n in range(cuts):
            part = pl.ds(n * (rows // cuts), rows // cuts)
            index = (0, part) if len(source.shape) == 3 else (part,)
            copies.append(pltpu.make_async_copy(
                source.at[index], target.at[index], sems.at[len(copies)]))
    for copy in copies:
        copy.start()
    for copy in copies:
        copy.wait()


def store(*arrays):
    return pl.pallas_call(
        store_kernel,
        out_shape=tuple(jax.ShapeDtypeStruct(a.shape, a.dtype) for a in arrays),
        in_specs=[pl.BlockSpec(memory_space=pltpu.VMEM)] * len(arrays),
        out_specs=tuple(pl.BlockSpec(memory_space=pltpu.HBM) for _ in arrays),
        scratch_shapes=[pltpu.SemaphoreType.DMA((3 * len(arrays),))],
        compiler_params=pltpu.CompilerParams(vmem_limit_bytes=2**20),
    )(*arrays)


def local(R, S, anchor, replica_rows, outer_velocity, features, cotangent,
          inner_weight, first_moment, second_moment):
    C, H = R // 2, SPLIT
    depth_rows = anchor.shape[0]
    W = outer_velocity.shape[1]
    f32, bf16 = jnp.float32, jnp.bfloat16
    args = (anchor, replica_rows, outer_velocity, features, cotangent,
            inner_weight, first_moment, second_moment)
    outs = (anchor, replica_rows, outer_velocity, inner_weight, first_moment, second_moment)
    dma = pltpu.SemaphoreType.DMA
    length = S // 2
    room = 67043328 - sum(a.size * a.dtype.itemsize for a in outs) - 2**16
    results = pl.pallas_call(
        functools.partial(kernel, R, S),
        out_shape=tuple(pltpu.VMEM(a.shape, a.dtype) for a in outs),
        in_specs=[pl.BlockSpec(memory_space=pltpu.HBM)] * len(args),
        out_specs=tuple(pl.BlockSpec(memory_space=pltpu.VMEM) for _ in outs),
        scratch_shapes=[
            pltpu.VMEM(anchor.shape, f32),
            pltpu.VMEM(replica_rows.shape[1:], bf16),
            pltpu.VMEM(outer_velocity.shape, f32),
            pltpu.VMEM(features.shape[1:], bf16),
            pltpu.VMEM((S * cotangent.shape[1], cotangent.shape[2]), bf16),
            pltpu.VMEM(inner_weight.shape[1:], f32),
            pltpu.VMEM(inner_weight.shape[1:], f32),
            pltpu.VMEM(inner_weight.shape[1:], f32),
            pltpu.VMEM((C, H, depth_rows, W // H), bf16),
            pltpu.VMEM((2, C, C, H, depth_rows, W // H), bf16),
            dma((7 + 2 * C,)),
            dma((C, H)),
            dma((C, H)),
            dma((C - 1, C, H)),
            dma((C, C, H)),
            dma((2, C, C, H)),
            dma((3, PARTS)),
            dma((2, max(length - 1, 1), PARTS)),
            dma((length, PARTS)),
            dma((S, PARTS)),
        ],
        compiler_params=pltpu.CompilerParams(
            collective_id=0, has_side_effects=True, vmem_limit_bytes=room),
    )(*args)
    return store(*results)


def solution(mesh):
    in_specs = (
        P("shard", None),
        P("replica", "shard", None),
        P("shard", "replica"),
        P("replica", "shard", None),
        P("replica", "shard", None),
        P("replica", "shard", None),
        P("replica", "shard", None),
        P("replica", "shard", None),
    )
    out_specs = (
        P("shard", None),
        P("replica", "shard", None),
        P("shard", "replica"),
        P("replica", "shard", None),
        P("replica", "shard", None),
        P("replica", "shard", None),
    )
    body = functools.partial(local, mesh.shape["replica"], mesh.shape["shard"])
    return jax.shard_map(body, mesh=mesh, in_specs=in_specs, out_specs=out_specs, check_vma=False)
```

profile of v0, /device:TPU:0, one launch (start us, length us, event | category | flops | bytes accessed | tf_op | source)
XLA Modules:
  0.0 21.2 jit_solution(2741369296660889941)
XLA Ops:
  0.6 18.7 %shard_map.127 = (f32[48,8192]{1,0:T(8,128)S(1)}, bf16[1,48,8192]{2,1,0:T(8,128)(2,1)S(1)}, f32[48,2048]{1,0:T(8,128)S(1)}, f32[1,48,1024]{2,1,0:T(8,128)S(1)}, ...) custom-call(f32[48,8192]{1,0:T(8,128)} %anchor_h.1, bf16[1,48,8192]{2,1,0:T(8,128)(2,1)} %rows_h.1, ...), custom_call_target="tpu_custom_call" | custom-call | tf_op jit(solution)/shard_map/pallas_call | solution.py:342
  19.3 1.9 %shard_map.128 = (f32[48,8192]{1,0:T(8,128)}, bf16[1,48,8192]{2,1,0:T(8,128)(2,1)}, f32[48,2048]{1,0:T(8,128)}, f32[1,48,1024]{2,1,0:T(8,128)}, f32[1,48,1024]{2,1,0:T(8,128)}, /*index=5*/f32[1,48,1024]{2,1,0:T(8,128)}) custom-call(f32[48,8192]{1,0:T(8,128)S(1)} %get-tuple-element.12.refs_0_, bf16[1,48,8192]{2,1,0:T(8,128)(2,1)S(1)} %get-tuple-element.13.refs_1_, ...), custom_call_target="tpu_custom_call" | custom-call | tf_op jit(solution)/shard_map/pallas_call | solution.py:320
where the time goes:
time: 21.3 us; the launch traced here: 21.2 us
  Pallas kernels  20.5 us (96%)
  between operations  0.64 us (3%)
    pallas_call x1, Pallas kernels, local(): pl.pallas_call(functools.partial(kernel, R, S), out_shape=tuple((pltpu.VM...  18.7 us
    pallas_call x1, Pallas kernels, store(): pl.pallas_call(store_kernel, out_shape=tuple((jax.ShapeDtypeStruct(a.shap...  1.87 us

commit v1 on v0

v1 whole, which is shorter than its diff:
```python
import functools

import jax
import jax.numpy as jnp
from jax import lax
from jax.experimental import pallas as pl
from jax.experimental.pallas import tpu as pltpu
from jax.sharding import PartitionSpec as P

momentum_keep = 0.9
outer_rate = 0.7
blend_keep = 0.5
inner_rate = 0.01
decay_first = 0.9
decay_second = 0.95
weight_decay = 0.1
epsilon = 1e-08
first_fix = 1.0 - 0.9**10
second_fix = 1.0 - 0.95**10

MESH = pl.DeviceIdType.MESH
SPLIT = 4
PARTS = 2
CUTS = 2


def kernel(R, S, anchor_h, rows_h, vel_h, feat_h, cot_h, w_h, m_h, s_h,
           na_o, mg_o, nv_o, nw_o, nm_o, ns_o,
           anchor, rows, vel, feat, cot, wms, sib_rows, msg,
           in_sem, sends, sib_recv, y_recv, own_recv, fwd_recv, z_recv, x_recv,
           ready_y, ready_x, ready_z):
    C, L, H = R // 2, S // 2, SPLIT
    me, at = lax.axis_index("replica"), lax.axis_index("shard")
    y, c = me // 2, me % 2
    pos, x = at // 2, at % 2
    sib = me + 1 - 2 * c
    partner = at + 1 - 2 * x
    W = vel.shape[1]
    piece = W // H
    depth = cot_h.shape[1]
    part_width = cot_h.shape[2] // PARTS

    def columns(q, h):
        return pl.ds(pl.multiple_of(q * W + h * piece, 128), piece)

    def quarter(q):
        return pl.ds(pl.multiple_of(q * W, 128), W)

    def tokens(k):
        return pl.ds(pl.multiple_of(k * depth, depth), depth)

    def block_part(k, u):
        return cot.at[tokens(k), pl.ds(u * part_width, part_width)]

    def tell(semaphore, **target):
        pl.semaphore_signal(semaphore, inc=1, device_id=target, device_id_type=MESH)

    barrier = pltpu.get_barrier_semaphore()
    tell(barrier, replica=sib)
    for t in range(1, C):
        @pl.when(y + t < C)
        def _():
            tell(barrier, replica=me + 2 * t)

    @pl.when(x == 0)
    def _():
        tell(barrier, shard=partner)

    for t in range(1, L):
        @pl.when(pos + t < L)
        def _():
            tell(barrier, shard=at + 2 * t)

    loads = {}

    def load(name, src, dst, slot=None):
        slot = len(loads) if slot is None else slot
        copy = pltpu.make_async_copy(src, dst, in_sem.at[slot])
        copy.start()
        loads[name] = copy

    for j in range(C):
        q = 2 * j + 1 - c
        load(("out", j), rows_h.at[0, :, quarter(q)], rows.at[:, quarter(q)])
    load("cot", cot_h.at[0], cot.at[tokens(at)])
    for j in range(C):
        q = 2 * j + c
        load(("keep", j), rows_h.at[0, :, quarter(q)], rows.at[:, quarter(q)])
    load("anchor", anchor_h, anchor)
    load("vel", vel_h, vel)
    load("feat", feat_h.at[0], feat)
    shared = len(loads)
    for n, source in enumerate((w_h, m_h, s_h)):
        load(("wms", n), source.at[0], wms.at[n], shared)

    pl.semaphore_wait(barrier, 1 + y + x + pos)
    for t in range(1, C):
        @pl.when(y >= t)
        def _():
            tell(ready_y, replica=me - 2 * t)

    @pl.when(x == 1)
    def _():
        tell(ready_x, shard=partner)

    for t in range(1, L):
        @pl.when(pos >= t)
        def _():
            tell(ready_z, shard=at - 2 * t)

    def remote(src, dst, send, recv, **target):
        return pltpu.make_async_remote_copy(
            src_ref=src, dst_ref=dst, send_sem=sends.at[send], recv_sem=recv,
            device_id=target, device_id_type=MESH)

    per = H // CUTS

    def sib_copy(j, g):
        q = 2 * j + 1 - c
        cols = pl.ds(pl.multiple_of(q * W + g * per * piece, 128), per * piece)
        return remote(rows.at[:, cols], sib_rows.at[j, g], 0, sib_recv.at[j, g], replica=sib)

    def cot_copy(k, u, recv, target):
        return remote(block_part(k, u), block_part(k, u), 2, recv, shard=target)

    for j in range(C):
        loads[("out", j)].wait()
        for g in range(CUTS):
            sib_copy(j, g).start()

    loads["cot"].wait()
    for t in range(L - 1, 0, -1):
        @pl.when(pos >= t)
        def _():
            for u in range(PARTS):
                cot_copy(at, u, z_recv.at[t - 1, u], at - 2 * t).start()

    def y_copy(t, j, h):
        return remote(msg.at[c * C + y, j, h], msg.at[c * C + y, j, h], 1,
                      y_recv.at[t - 1, j, h], replica=lax.rem(me + 2 * t, R))

    def own_to_sib(j, h):
        return remote(msg.at[c * C + y, j, h], msg.at[c * C + y, j, h], 1, own_recv, replica=sib)

    def to_sib(t, j, h):
        slot = c * C + lax.rem(y + C - t, C)
        return remote(msg.at[slot, j, h], msg.at[slot, j, h], 1, fwd_recv.at[t - 1, j, h], replica=sib)

    c1 = outer_rate * (1.0 + momentum_keep)
    c2 = outer_rate * momentum_keep * momentum_keep
    share = c1 / R
    for j in range(C):
        loads[("keep", j)].wait()
        if j == 0:
            loads["anchor"].wait()
            loads["vel"].wait()
        mine = y == j
        of_anchor = jnp.where(mine, 0.0, 2.0)
        of_rows = jnp.where(mine, share, -1.0)
        of_vel = jnp.where(mine, -c2, 0.0)
        for h in range(H):
            if h % per == 0:
                sib_copy(j, h // per).wait_recv()
            cols = columns(2 * j + c, h)
            inner = pl.ds(h % per * piece, piece)
            both = rows[:, cols].astype(jnp.float32) + sib_rows[j, h // per, :, inner].astype(jnp.float32)
            value = of_anchor * anchor[:, cols] + of_rows * both
            value = value + of_vel * vel[:, h * piece:(h + 1) * piece]
            msg[c * C + y, j, h] = value.astype(jnp.bfloat16)
            if j == 0 and h == 0:
                @pl.when(y < C - 1)
                def _():
                    pl.semaphore_wait(ready_y, C - 1 - y)

            for t in range(1, C):
                y_copy(t, j, h).start()
            own_to_sib(j, h).start()

    @pl.when(x == 0)
    def _():
        pl.semaphore_wait(ready_x, 1)

    for u in range(PARTS):
        cot_copy(at, u, x_recv, partner).start()

    @pl.when(pos < L - 1)
    def _():
        pl.semaphore_wait(ready_z, L - 1 - pos)

    for t in range(L - 1, 0, -1):
        @pl.when(pos + t < L)
        def _():
            for u in range(PARTS):
                cot_copy(at, u, z_recv.at[L - t - 1, u], at + 2 * t).start()

    def finish(p, j, h):
        cols = columns(2 * j + p, h)
        others = msg[p * C + (j + 1) % C, j, h].astype(jnp.float32)
        for t in range(2, C):
            others = others + msg[p * C + (j + t) % C, j, h].astype(jnp.float32)
        own = msg[p * C + j, j, h].astype(jnp.float32)
        new_anchor = (1.0 - 2.0 * share) * anchor[:, cols] + own - share * others
        na_o[:, cols] = new_anchor
        mg_o[0, :, cols] = (
            blend_keep * rows[:, cols].astype(jnp.float32) + (1.0 - blend_keep) * new_anchor
        ).astype(jnp.bfloat16)

    def finish_velocity(j, h):
        @pl.when(y == j)
        def _():
            cols = columns(2 * j + c, h)
            part = slice(h * piece, (h + 1) * piece)
            inner = pl.ds(h % per * piece, piece)
            total = 2.0 * anchor[:, cols] - (
                rows[:, cols].astype(jnp.float32) + sib_rows[j, h // per, :, inner].astype(jnp.float32))
            for t in range(1, C):
                total = total + msg[c * C + (j + t) % C, j, h].astype(jnp.float32)
            nv_o[:, part] = momentum_keep * vel[:, part] + total / R

    def whole(ref, recv):
        return pltpu.make_async_remote_copy(
            src_ref=ref, dst_ref=ref, send_sem=recv, recv_sem=recv,
            device_id={"replica": sib}, device_id_type=MESH)

    def finish_sib(j, h):
        for t in range(1, C):
            to_sib(t, j, h).wait_recv()
        finish(1 - c, j, h)

    def own_piece(j, h):
        for t in range(1, C):
            y_copy(t, j, h).wait_recv()
            to_sib(t, j, h).start()
        finish(c, j, h)
        finish_velocity(j, h)

    def cot_piece(i, u):
        higher = L - 1 - pos
        d = jnp.where(i < higher, i + 1, L - 1 - (i - higher))
        k = 2 * lax.rem(pos + d, L) + x
        cot_copy(k, u, z_recv.at[d - 1, u], partner).wait_recv()
        cot_copy(k, u, x_recv, partner).start()

    def inner_step():
        whole(cot.at[:L * depth], x_recv).wait_recv()
        loads["feat"].wait()
        pltpu.make_async_copy(wms, wms, in_sem.at[shared]).wait()
        tile = min(256, nw_o.shape[2])
        for n in range(nw_o.shape[2] // tile):
            part = slice(n * tile, (n + 1) * tile)
            gradient = jnp.dot(feat[...], cot[:, part], preferred_element_type=jnp.float32)
            new_first = decay_first * wms[1, :, part] + (1.0 - decay_first) * gradient
            new_second = decay_second * wms[2, :, part] + (1.0 - decay_second) * gradient * gradient
            stepped = new_first / first_fix / (jnp.sqrt(new_second / second_fix) + epsilon)
            weight = wms[0, :, part]
            nw_o[0, :, part] = weight - inner_rate * (stepped + weight_decay * weight)
            nm_o[0, :, part] = new_first
            ns_o[0, :, part] = new_second

    pieces = [(j, h) for j in range(C) for h in range(H)]
    todo = [(i, u) for i in range(L - 1) for u in range(PARTS)]
    each = PARTS * -(-(L - 1) // max(len(pieces) - 5, 1))
    late = len(pieces) - 2
    for i, (j, h) in enumerate(pieces):
        if i == late:
            inner_step()
        own_piece(j, h)
        if i == 1:
            whole(msg.at[0], own_recv).wait_recv()
        if i >= 1:
            finish_sib(*pieces[i - 1])
        for step in todo[i * each:(i + 1) * each]:
            cot_piece(*step)
    finish_sib(*pieces[-1])

    whole(sib_rows, sends.at[0]).wait_send()
    whole(msg.at[:2 * C - 1], sends.at[1]).wait_send()
    whole(cot.at[:(2 * L - 1) * depth], sends.at[2]).wait_send()


def store_kernel(*refs):
    sems = refs[-1]
    count = (len(refs) - 1) // 2
    pairs = list(zip(refs[:count], refs[count:-1]))
    for i, (source, target) in enumerate(pairs):
        rows = source.shape[-2]
        cuts = 3 if rows % 48 == 0 else 1
        for n in range(cuts):
            part = pl.ds(n * (rows // cuts), rows // cuts)
            index = (0, part) if len(source.shape) == 3 else (part,)
            pltpu.make_async_copy(source.at[index], target.at[index], sems.at[i]).start()
    for i, (source, target) in enumerate(pairs):
        pltpu.make_async_copy(source, target, sems.at[i]).wait()


def store(*arrays):
    return pl.pallas_call(
        store_kernel,
        out_shape=tuple(jax.ShapeDtypeStruct(a.shape, a.dtype) for a in arrays),
        in_specs=[pl.BlockSpec(memory_space=pltpu.VMEM)] * len(arrays),
        out_specs=tuple(pl.BlockSpec(memory_space=pltpu.HBM) for _ in arrays),
        scratch_shapes=[pltpu.SemaphoreType.DMA((len(arrays),))],
        compiler_params=pltpu.CompilerParams(vmem_limit_bytes=2**20),
    )(*arrays)


def local(R, S, anchor, replica_rows, outer_velocity, features, cotangent,
          inner_weight, first_moment, second_moment):
    C, L, H = R // 2, S // 2, SPLIT
    height = anchor.shape[0]
    W = outer_velocity.shape[1]
    f32, bf16 = jnp.float32, jnp.bfloat16
    args = (anchor, replica_rows, outer_velocity, features, cotangent,
            inner_weight, first_moment, second_moment)
    outs = (anchor, replica_rows, outer_velocity, inner_weight, first_moment, second_moment)
    dma, regular = pltpu.SemaphoreType.DMA, pltpu.SemaphoreType.REGULAR
    room = 67043328 - sum(a.size * a.dtype.itemsize for a in outs) - 2**16
    results = pl.pallas_call(
        functools.partial(kernel, R, S),
        out_shape=tuple(pltpu.VMEM(a.shape, a.dtype) for a in outs),
        in_specs=[pl.BlockSpec(memory_space=pltpu.HBM)] * len(args),
        out_specs=tuple(pl.BlockSpec(memory_space=pltpu.VMEM) for _ in outs),
        scratch_shapes=[
            pltpu.VMEM(anchor.shape, f32),
            pltpu.VMEM(replica_rows.shape[1:], bf16),
            pltpu.VMEM(outer_velocity.shape, f32),
            pltpu.VMEM(features.shape[1:], bf16),
            pltpu.VMEM((S * cotangent.shape[1], cotangent.shape[2]), bf16),
            pltpu.VMEM((3,) + inner_weight.shape[1:], f32),
            pltpu.VMEM((C, CUTS, height, W // CUTS), bf16),
            pltpu.VMEM((2 * C, C, H, height, W // H), bf16),
            dma((5 + 2 * C,)),
            dma((3,)),
            dma((C, CUTS)),
            dma((C - 1, C, H)),
            dma,
            dma((C - 1, C, H)),
            dma((max(L - 1, 1), PARTS)),
            dma,
            regular,
            regular,
            regular,
        ],
        compiler_params=pltpu.CompilerParams(
            collective_id=0, has_side_effects=True, vmem_limit_bytes=room),
    )(*args)
    return store(*results)


def solution(mesh):
    in_specs = (
        P("shard", None),
        P("replica", "shard", None),
        P("shard", "replica"),
        P("replica", "shard", None),
        P("replica", "shard", None),
        P("replica", "shard", None),
        P("replica", "shard", None),
        P("replica", "shard", None),
    )
    out_specs = (
        P("shard", None),
        P("replica", "shard", None),
        P("shard", "replica"),
        P("replica", "shard", None),
        P("replica", "shard", None),
        P("replica", "shard", None),
    )
    body = functools.partial(local, mesh.shape["replica"], mesh.shape["shard"])
    return jax.shard_map(body, mesh=mesh, in_specs=in_specs, out_specs=out_specs, check_vma=False)
```

time: 21.3 us -> 19.3 us (0.906); the launches traced: 21.2 us -> 18.9 us
  Pallas kernels: 20.5 us -> 18.3 us
    pallas_call x1, Pallas kernels: 18.7 us -> 16.5 us  [local(): pl.pallas_call(functools.partial(kernel, R, S), out_shape=tuple((pltpu.VM...]
where the time goes in v1:
time: 19.3 us; the launch traced here: 18.9 us
  Pallas kernels  18.3 us (95%)
  between operations  0.64 us (3%)
    pallas_call x1, Pallas kernels, local(): pl.pallas_call(functools.partial(kernel, R, S), out_shape=tuple((pltpu.VM...  16.5 us
    pallas_call x1, Pallas kernels, store(): pl.pallas_call(store_kernel, out_shape=tuple((jax.ShapeDtypeStruct(a.shap...  1.76 us

profile of v1, /device:TPU:0, one launch (start us, length us, event | category | flops | bytes accessed | tf_op | source)
XLA Modules:
  0.0 18.9 jit_solution(16165282919922946209)
XLA Ops:
  0.6 16.5 %shard_map.127 = (f32[48,8192]{1,0:T(8,128)S(1)}, bf16[1,48,8192]{2,1,0:T(8,128)(2,1)S(1)}, f32[48,2048]{1,0:T(8,128)S(1)}, f32[1,48,1024]{2,1,0:T(8,128)S(1)}, ...) custom-call(f32[48,8192]{1,0:T(8,128)} %anchor_h.1, bf16[1,48,8192]{2,1,0:T(8,128)(2,1)} %rows_h.1, ...), custom_call_target="tpu_custom_call" | custom-call | tf_op jit(solution)/shard_map/pallas_call | solution.py:318
  17.2 1.8 %shard_map.128 = (f32[48,8192]{1,0:T(8,128)}, bf16[1,48,8192]{2,1,0:T(8,128)(2,1)}, f32[48,2048]{1,0:T(8,128)}, f32[1,48,1024]{2,1,0:T(8,128)}, f32[1,48,1024]{2,1,0:T(8,128)}, /*index=5*/f32[1,48,1024]{2,1,0:T(8,128)}) custom-call(f32[48,8192]{1,0:T(8,128)S(1)} %get-tuple-element.12.refs_0_, bf16[1,48,8192]{2,1,0:T(8,128)(2,1)S(1)} %get-tuple-element.13.refs_1_, ...), custom_call_target="tpu_custom_call" | custom-call | tf_op jit(solution)/shard_map/pallas_call | solution.py:297

commit v2 on v1

v2 whole, which is shorter than its diff:
```python
import functools

import jax
import jax.numpy as jnp
from jax import lax
from jax.experimental import pallas as pl
from jax.experimental.pallas import tpu as pltpu
from jax.sharding import PartitionSpec as P

momentum_keep = 0.9
outer_rate = 0.7
blend_keep = 0.5
inner_rate = 0.01
decay_first = 0.9
decay_second = 0.95
weight_decay = 0.1
epsilon = 1e-08
first_fix = 1.0 - 0.9**10
second_fix = 1.0 - 0.95**10

MESH = pl.DeviceIdType.MESH
SPLIT = 4
PARTS = 4
CUTS = 2
EXTRA = 1
LAG = 3


def kernel(R, S, anchor_h, rows_h, vel_h, feat_h, cot_h, w_h, m_h, s_h,
           na_o, mg_o, nv_o, nw_o, nm_o, ns_o,
           anchor, rows, vel, feat, cot, wms, sib_rows, more_rows, more_vel, msg,
           in_sem, sends, sib_recv, more_recv, y_recv, more_y, own_recv, fwd_recv, high_fwd, more_fwd,
           z_recv, x_recv, ready_y, ready_x, ready_z):
    C, L, H = R // 2, S // 2, SPLIT
    LOW = H - EXTRA
    me, at = lax.axis_index("replica"), lax.axis_index("shard")
    y, c = me // 2, me % 2
    pos, x = at // 2, at % 2
    sib = me + 1 - 2 * c
    partner = at + 1 - 2 * x
    W = vel.shape[1]
    piece = W // H
    per = H // CUTS
    depth = cot_h.shape[1]
    part_width = cot_h.shape[2] // PARTS
    c1 = outer_rate * (1.0 + momentum_keep)
    c2 = outer_rate * momentum_keep * momentum_keep
    share = c1 / R

    def columns(q, h, count=1):
        return pl.ds(pl.multiple_of(q * W + h * piece, 128), count * piece)

    def quarter(q):
        return columns(q, 0, H)

    def tokens(k):
        return pl.ds(pl.multiple_of(k * depth, depth), depth)

    def turn(r):
        return lax.rem(y + r, C)

    def tell(semaphore, **target):
        pl.semaphore_signal(semaphore, inc=1, device_id=target, device_id_type=MESH)

    barrier = pltpu.get_barrier_semaphore()
    tell(barrier, replica=sib)
    for t in range(1, C):
        @pl.when(y + t < C)
        def _():
            tell(barrier, replica=me + 2 * t)

    @pl.when(x == 0)
    def _():
        tell(barrier, shard=partner)

    for t in range(1, L):
        @pl.when(pos + t < L)
        def _():
            tell(barrier, shard=at + 2 * t)

    OUT, COT, VEL, FEAT, WMS, REST, KEEP = 0, 1, 2, 3, 4, 5, 6
    NEAR = KEEP + C

    def load(src, dst, slot):
        copy = pltpu.make_async_copy(src, dst, in_sem.at[slot])
        copy.start()
        return copy

    for r in range(C):
        cols = quarter(2 * turn(r) + 1 - c)
        load(rows_h.at[0, :, cols], rows.at[:, cols], OUT)
    cot_load = load(cot_h.at[0], cot.at[tokens(at)], COT)
    keep_load, near_load = [], []
    for r in range(C):
        cols = quarter(2 * turn(r) + c)
        keep_load.append(load(rows_h.at[0, :, cols], rows.at[:, cols], KEEP + r))
        if r == 0:
            vel_load = load(vel_h, vel, VEL)
        else:
            near_load.append(load(anchor_h.at[:, cols], anchor.at[:, cols], NEAR + r - 1))

    pl.semaphore_wait(barrier, 1 + y + x + pos)
    for t in range(1, C):
        @pl.when(y >= t)
        def _():
            tell(ready_y, replica=me - 2 * t)

    @pl.when(x == 1)
    def _():
        tell(ready_x, shard=partner)

    for t in range(1, L):
        @pl.when(pos >= t)
        def _():
            tell(ready_z.at[t - 1], shard=at - 2 * t)

    def remote(src, dst, send, recv, **target):
        return pltpu.make_async_remote_copy(
            src_ref=src, dst_ref=dst, send_sem=sends.at[send], recv_sem=recv,
            device_id=target, device_id_type=MESH)

    def whole(ref, semaphore):
        return pltpu.make_async_remote_copy(
            src_ref=ref, dst_ref=ref, send_sem=semaphore, recv_sem=semaphore,
            device_id={"replica": sib}, device_id_type=MESH)

    def sib_copy(j, g):
        cols = columns(2 * j + 1 - c, g * per, per)
        return remote(rows.at[:, cols], sib_rows.at[j, g], 0, sib_recv.at[j, g], replica=sib)

    def more_copy(j):
        cols = columns(2 * j, LOW, EXTRA)
        return remote(rows.at[:, cols], more_rows.at[j], 0, more_recv.at[0], replica=sib)

    def more_vel_copy():
        return remote(vel.at[:, pl.ds(LOW * piece, EXTRA * piece)], more_vel, 0, more_recv.at[1], replica=sib)

    def cot_copy(k, u, recv, target):
        block = cot.at[tokens(k), pl.ds(u * part_width, part_width)]
        return remote(block, block, 2, recv, shard=target)

    def left_sends():
        for t in range(L - 1, 0, -1):
            @pl.when(pos >= t)
            def _():
                for u in range(PARTS):
                    cot_copy(at, u, z_recv.at[t - 1, u], at - 2 * t).start()

    pltpu.make_async_copy(rows_h.at[0, :, pl.ds(0, C * W)], rows.at[:, pl.ds(0, C * W)], in_sem.at[OUT]).wait()
    for r in range(C):
        for g in range(CUTS):
            sib_copy(turn(r), g).start()
    for q in [2 * turn(0) + c] + [2 * turn(r) + 1 - c for r in range(C)]:
        load(anchor_h.at[:, quarter(q)], anchor.at[:, quarter(q)], REST)
    load(feat_h.at[0], feat, FEAT)
    for n, source in enumerate((w_h, m_h, s_h)):
        load(source.at[0], wms.at[n], WMS)
    cot_load.wait()
    pl.when(c == 0)(left_sends)

    def slot(p, src, j, h):
        return ((p * C + src) * C + j) * H + h

    def message(p, src, j, h):
        return msg.at[slot(p, src, j, h)]

    def y_copy(t, p, j, h, recv):
        return remote(message(p, y, j, h), message(p, y, j, h), 1, recv, replica=lax.rem(me + 2 * t, R))

    def own_to_sib(p, j, h):
        return remote(message(p, y, j, h), message(p, y, j, h), 1, own_recv, replica=sib)

    def to_sib(t, p, j, h, recv):
        src = lax.rem(y + C - t, C)
        return remote(message(p, src, j, h), message(p, src, j, h), 1, recv, replica=sib)

    def add_message(p, r, h, other_rows, velocity):
        j = turn(r)
        cols = columns(2 * j + p, h)
        both = rows[:, cols].astype(jnp.float32) + other_rows.astype(jnp.float32)
        if r == 0:
            value = share * both - c2 * velocity
        else:
            value = 2.0 * anchor[:, cols] - both
        msg[slot(p, y, j, h)] = value.astype(jnp.bfloat16)

    def from_sib(j, h):
        return sib_rows[j, h // per, :, pl.ds(h % per * piece, piece)]

    for r in range(C):
        j = turn(r)
        keep_load[r].wait()

        @pl.when(c == 0)
        def _():
            more_copy(j).start()

        if r == 0:
            vel_load.wait()

            @pl.when(c == 0)
            def _():
                more_vel_copy().start()
        else:
            near_load[r - 1].wait()

        for h in range(H):
            if h % per == 0:
                sib_copy(j, h // per).wait_recv()

            def handle():
                add_message(c, r, h, from_sib(j, h), vel[:, h * piece:(h + 1) * piece])
                if r == 0 and h == 0:
                    @pl.when(y < C - 1)
                    def _():
                        pl.semaphore_wait(ready_y, C - 1 - y)

                for t in range(1, C):
                    y_copy(t, c, j, h, y_recv.at[t - 1, r, h]).start()
                own_to_sib(c, j, h).start()

            if h < LOW:
                handle()
            else:
                pl.when(c == 1)(handle)

    pl.when(c == 1)(left_sends)

    @pl.when(x == 0)
    def _():
        pl.semaphore_wait(ready_x, 1)

    for u in range(PARTS):
        cot_copy(at, u, x_recv, partner).start()

    pltpu.make_async_copy(
        anchor_h.at[:, pl.ds(0, (C + 1) * W)], anchor.at[:, pl.ds(0, (C + 1) * W)], in_sem.at[REST]).wait()

    @pl.when(c == 1)
    def _():
        whole(more_rows, more_recv.at[0]).wait_recv()
        more_vel_copy().wait_recv()
        for r in range(C):
            for n in range(EXTRA):
                h, inner = LOW + n, pl.ds(n * piece, piece)
                add_message(0, r, h, more_rows[turn(r), :, inner], more_vel[:, inner])
                for t in range(1, C):
                    y_copy(t, 0, turn(r), h, more_y.at[t - 1, r, n]).start()
                own_to_sib(0, turn(r), h).start()

    for t in range(1, L):
        @pl.when(pos + t < L)
        def _():
            pl.semaphore_wait(ready_z.at[t - 1], 1)
            for u in range(PARTS):
                cot_copy(at, u, z_recv.at[L - t - 1, u], at + 2 * t).start()

    def finish(p, j, h):
        cols = columns(2 * j + p, h)
        others = msg[slot(p, lax.rem(j + 1, C), j, h)].astype(jnp.float32)
        for t in range(2, C):
            others = others + msg[slot(p, lax.rem(j + t, C), j, h)].astype(jnp.float32)
        own = msg[slot(p, j, j, h)].astype(jnp.float32)
        new_anchor = (1.0 - 2.0 * share) * anchor[:, cols] + own - share * others
        na_o[:, cols] = new_anchor
        mg_o[0, :, cols] = (
            blend_keep * rows[:, cols].astype(jnp.float32) + (1.0 - blend_keep) * new_anchor
        ).astype(jnp.bfloat16)

    def finish_velocity(r, h):
        if r == C - 1:
            cols = columns(2 * y + c, h)
            part = slice(h * piece, (h + 1) * piece)
            total = 2.0 * anchor[:, cols] - (
                rows[:, cols].astype(jnp.float32) + from_sib(y, h).astype(jnp.float32))
            for t in range(1, C):
                total = total + msg[slot(c, lax.rem(y + t, C), y, h)].astype(jnp.float32)
            nv_o[:, part] = momentum_keep * vel[:, part] + total / R

    def came(r):
        return turn(r + 1)

    def sent(r, t):
        return (r + 1 + t) % C

    def own_piece(r, h, forward):
        for t in range(1, C):
            y_copy(t, c, came(r), h, y_recv.at[t - 1, sent(r, t), h]).wait_recv()
            to_sib(t, c, came(r), h, forward).start()
        finish(c, came(r), h)
        finish_velocity(r, h)

    def more_piece(r, n):
        for t in range(1, C):
            y_copy(t, 0, came(r), LOW + n, more_y.at[t - 1, sent(r, t), n]).wait_recv()
            to_sib(t, 0, came(r), LOW + n, more_fwd).start()
        finish(0, came(r), LOW + n)

    def pieces_from_sib(n, semaphore):
        whole(msg.at[:n], semaphore).wait_recv()

    def low_group(r):
        pieces_from_sib((C - 1) * LOW, fwd_recv.at[r])
        for h in range(LOW):
            finish(1 - c, came(r), h)

    def cot_piece(i, u):
        higher = L - 1 - pos
        d = jnp.where(i < higher, i + 1, L - 1 - (i - higher))
        k = 2 * lax.rem(pos + d, L) + x
        cot_copy(k, u, z_recv.at[d - 1, u], partner).wait_recv()
        cot_copy(k, u, x_recv, partner).start()

    def inner_step():
        whole(cot.at[:L * depth], x_recv).wait_recv()
        pltpu.make_async_copy(feat_h.at[0], feat, in_sem.at[FEAT]).wait()
        pltpu.make_async_copy(wms, wms, in_sem.at[WMS]).wait()
        tile = min(256, nw_o.shape[2])
        for n in range(nw_o.shape[2] // tile):
            part = slice(n * tile, (n + 1) * tile)
            gradient = jnp.dot(feat[...], cot[:, part], preferred_element_type=jnp.float32)
            new_first = decay_first * wms[1, :, part] + (1.0 - decay_first) * gradient
            new_second = decay_second * wms[2, :, part] + (1.0 - decay_second) * gradient * gradient
            stepped = new_first / first_fix / (jnp.sqrt(new_second / second_fix) + epsilon)
            weight = wms[0, :, part]
            nw_o[0, :, part] = weight - inner_rate * (stepped + weight_decay * weight)
            nm_o[0, :, part] = new_first
            ns_o[0, :, part] = new_second

    low = [(r, h) for r in range(C) for h in range(LOW)]
    todo = [(i, u) for i in range(L - 1) for u in range(PARTS)]
    each = PARTS * -(-(L - 1) // max(len(low) - 2, 1))
    ready = []
    for i, (r, h) in enumerate(low):
        for step in todo[i * each:(i + 1) * each]:
            cot_piece(*step)
        own_piece(r, h, fwd_recv.at[r])
        if i == LAG - 1:
            @pl.when(c == 0)
            def _():
                pieces_from_sib(C * (H + EXTRA), own_recv)

            @pl.when(c == 1)
            def _():
                pieces_from_sib(C * LOW, own_recv)

        if h == LOW - 1:
            ready.append(r)
        if len(ready) > 1 and h == LOW - 2:
            low_group(ready.pop(0))

    @pl.when(c == 1)
    def _():
        for r in range(C):
            for h in range(LOW, H):
                own_piece(r, h, high_fwd)
        for r in ready:
            low_group(r)
        for r in range(C):
            for n in range(EXTRA):
                more_piece(r, n)
        inner_step()

    @pl.when(c == 0)
    def _():
        for r in ready:
            low_group(r)
        pieces_from_sib((C - 1) * C * EXTRA, high_fwd)
        for r in range(C):
            for h in range(LOW, H):
                finish(1, came(r), h)
        inner_step()
        pieces_from_sib((C - 1) * C * EXTRA, more_fwd)
        for r in range(C):
            for h in range(LOW, H):
                finish(0, came(r), h)
                finish_velocity(r, h)

    whole(cot.at[:(2 * L - 1) * depth], sends.at[2]).wait_send()

    @pl.when(c == 0)
    def _():
        whole(rows.at[:, pl.ds(0, (C * (H + EXTRA) + 2 * EXTRA) * piece)], sends.at[0]).wait_send()
        whole(msg.at[:(2 * C - 1) * C * LOW], sends.at[1]).wait_send()

    @pl.when(c == 1)
    def _():
        whole(sib_rows, sends.at[0]).wait_send()
        whole(msg.at[:(2 * C - 1) * C * (H + EXTRA)], sends.at[1]).wait_send()


def store_kernel(*refs):
    sems = refs[-1]
    count = (len(refs) - 1) // 2
    pairs = list(zip(refs[:count], refs[count:-1]))
    for i, (source, target) in enumerate(pairs):
        rows = source.shape[-2]
        cuts = 3 if rows % 48 == 0 else 1
        for n in range(cuts):
            part = pl.ds(n * (rows // cuts), rows // cuts)
            index = (0, part) if len(source.shape) == 3 else (part,)
            pltpu.make_async_copy(source.at[index], target.at[index], sems.at[i]).start()
    for i, (source, target) in enumerate(pairs):
        pltpu.make_async_copy(source, target, sems.at[i]).wait()


def store(*arrays):
    return pl.pallas_call(
        store_kernel,
        out_shape=tuple(jax.ShapeDtypeStruct(a.shape, a.dtype) for a in arrays),
        in_specs=[pl.BlockSpec(memory_space=pltpu.VMEM)] * len(arrays),
        out_specs=tuple(pl.BlockSpec(memory_space=pltpu.HBM) for _ in arrays),
        scratch_shapes=[pltpu.SemaphoreType.DMA((len(arrays),))],
        compiler_params=pltpu.CompilerParams(vmem_limit_bytes=2**20),
    )(*arrays)


def local(R, S, anchor, replica_rows, outer_velocity, features, cotangent,
          inner_weight, first_moment, second_moment):
    C, L, H = R // 2, S // 2, SPLIT
    height = anchor.shape[0]
    W = outer_velocity.shape[1]
    f32, bf16 = jnp.float32, jnp.bfloat16
    args = (anchor, replica_rows, outer_velocity, features, cotangent,
            inner_weight, first_moment, second_moment)
    outs = (anchor, replica_rows, outer_velocity, inner_weight, first_moment, second_moment)
    dma, regular = pltpu.SemaphoreType.DMA, pltpu.SemaphoreType.REGULAR
    room = 67043328 - sum(a.size * a.dtype.itemsize for a in outs) - 2**16
    results = pl.pallas_call(
        functools.partial(kernel, R, S),
        out_shape=tuple(pltpu.VMEM(a.shape, a.dtype) for a in outs),
        in_specs=[pl.BlockSpec(memory_space=pltpu.HBM)] * len(args),
        out_specs=tuple(pl.BlockSpec(memory_space=pltpu.VMEM) for _ in outs),
        scratch_shapes=[
            pltpu.VMEM(anchor.shape, f32),
            pltpu.VMEM(replica_rows.shape[1:], bf16),
            pltpu.VMEM(outer_velocity.shape, f32),
            pltpu.VMEM(features.shape[1:], bf16),
            pltpu.VMEM((S * cotangent.shape[1], cotangent.shape[2]), bf16),
            pltpu.VMEM((3,) + inner_weight.shape[1:], f32),
            pltpu.VMEM((C, CUTS, height, W // CUTS), bf16),
            pltpu.VMEM((C, height, EXTRA * (W // H)), bf16),
            pltpu.VMEM((height, EXTRA * (W // H)), f32),
            pltpu.VMEM((2 * C * C * (H + EXTRA), height, W // H), bf16),
            dma((5 + 2 * C,)),
            dma((3,)),
            dma((C, CUTS)),
            dma((2,)),
            dma((C - 1, C, H)),
            dma((C - 1, C, EXTRA)),
            dma,
            dma((C,)),
            dma,
            dma,
            dma((max(L - 1, 1), PARTS)),
            dma,
            regular,
            regular,
            regular((max(L - 1, 1),)),
        ],
        compiler_params=pltpu.CompilerParams(
            collective_id=0, has_side_effects=True, vmem_limit_bytes=room),
    )(*args)
    return store(*results)


def solution(mesh):
    in_specs = (
        P("shard", None),
        P("replica", "shard", None),
        P("shard", "replica"),
        P("replica", "shard", None),
        P("replica", "shard", None),
        P("replica", "shard", None),
        P("replica", "shard", None),
        P("replica", "shard", None),
    )
    out_specs = (
        P("shard", None),
        P("replica", "shard", None),
        P("shard", "replica"),
        P("replica", "shard", None),
        P("replica", "shard", None),
        P("replica", "shard", None),
    )
    body = functools.partial(local, mesh.shape["replica"], mesh.shape["shard"])
    return jax.shard_map(body, mesh=mesh, in_specs=in_specs, out_specs=out_specs, check_vma=False)
```

time: 19.3 us -> 18.4 us (0.953); the launches traced: 18.9 us -> 18.2 us
  Pallas kernels: 18.3 us -> 17.6 us
    pallas_call x1, Pallas kernels: 16.5 us -> 15.8 us  [local(): pl.pallas_call(functools.partial(kernel, R, S), out_shape=tuple((pltpu.VM...]
where the time goes in v2:
time: 18.4 us; the launch traced here: 18.2 us
  Pallas kernels  17.6 us (96%)
  between operations  0.64 us (3%)
    pallas_call x1, Pallas kernels, local(): pl.pallas_call(functools.partial(kernel, R, S), out_shape=tuple((pltpu.VM...  15.8 us
    pallas_call x1, Pallas kernels, store(): pl.pallas_call(store_kernel, out_shape=tuple((jax.ShapeDtypeStruct(a.shap...  1.76 us

profile of v2, /device:TPU:0, one launch (start us, length us, event | category | flops | bytes accessed | tf_op | source)
XLA Modules:
  0.0 18.2 jit_solution(13151702689037511544)
XLA Ops:
  0.6 15.8 %shard_map.127 = (f32[48,8192]{1,0:T(8,128)S(1)}, bf16[1,48,8192]{2,1,0:T(8,128)(2,1)S(1)}, f32[48,2048]{1,0:T(8,128)S(1)}, f32[1,48,1024]{2,1,0:T(8,128)S(1)}, ...) custom-call(f32[48,8192]{1,0:T(8,128)} %anchor_h.1, bf16[1,48,8192]{2,1,0:T(8,128)(2,1)} %rows_h.1, ...), custom_call_target="tpu_custom_call" | custom-call | tf_op jit(solution)/shard_map/pallas_call | solution.py:429
  16.5 1.8 %shard_map.128 = (f32[48,8192]{1,0:T(8,128)}, bf16[1,48,8192]{2,1,0:T(8,128)(2,1)}, f32[48,2048]{1,0:T(8,128)}, f32[1,48,1024]{2,1,0:T(8,128)}, f32[1,48,1024]{2,1,0:T(8,128)}, /*index=5*/f32[1,48,1024]{2,1,0:T(8,128)}) custom-call(f32[48,8192]{1,0:T(8,128)S(1)} %get-tuple-element.12.refs_0_, bf16[1,48,8192]{2,1,0:T(8,128)(2,1)S(1)} %get-tuple-element.13.refs_1_, ...), custom_call_target="tpu_custom_call" | custom-call | tf_op jit(solution)/shard_map/pallas_call | solution.py:408

commit v3 on v2

--- a/solution.py
+++ b/solution.py
@@ -78,7 +78,7 @@
         def _():
             tell(barrier, shard=at + 2 * t)
 
-    OUT, COT, VEL, FEAT, WMS, REST, KEEP = 0, 1, 2, 3, 4, 5, 6
+    FIRST, OUT, COT, VEL, FEAT, WMS, REST, KEEP = range(8)
     NEAR = KEEP + C
 
     def load(src, dst, slot):
@@ -87,8 +87,9 @@
         return copy
 
     for r in range(C):
-        cols = quarter(2 * turn(r) + 1 - c)
-        load(rows_h.at[0, :, cols], rows.at[:, cols], OUT)
+        for g in range(CUTS):
+            cols = columns(2 * turn(r) + 1 - c, g * per, per)
+            load(rows_h.at[0, :, cols], rows.at[:, cols], OUT if r or g else FIRST)
     cot_load = load(cot_h.at[0], cot.at[tokens(at)], COT)
     keep_load, near_load = [], []
     for r in range(C):
@@ -141,15 +142,22 @@
 
     def left_sends():
         for t in range(L - 1, 0, -1):
-            @pl.when(pos >= t)
+            @pl.when((pos >= 1) if t == 1 else (pos == L - 1))
             def _():
                 for u in range(PARTS):
                     cot_copy(at, u, z_recv.at[t - 1, u], at - 2 * t).start()
 
-    pltpu.make_async_copy(rows_h.at[0, :, pl.ds(0, C * W)], rows.at[:, pl.ds(0, C * W)], in_sem.at[OUT]).wait()
+    def loaded(count, semaphore):
+        cols = pl.ds(0, count * piece)
+        pltpu.make_async_copy(rows_h.at[0, :, cols], rows.at[:, cols], in_sem.at[semaphore]).wait()
+
+    loaded(per, FIRST)
+    sib_copy(turn(0), 0).start()
+    loaded(C * H - per, OUT)
     for r in range(C):
         for g in range(CUTS):
-            sib_copy(turn(r), g).start()
+            if r or g:
+                sib_copy(turn(r), g).start()
     for q in [2 * turn(0) + c] + [2 * turn(r) + 1 - c for r in range(C)]:
         load(anchor_h.at[:, quarter(q)], anchor.at[:, quarter(q)], REST)
     load(feat_h.at[0], feat, FEAT)
@@ -224,7 +232,8 @@
             else:
                 pl.when(c == 1)(handle)
 
-    pl.when(c == 1)(left_sends)
+        if r == 0:
+            pl.when(c == 1)(left_sends)
 
     @pl.when(x == 0)
     def _():
@@ -252,6 +261,9 @@
         @pl.when(pos + t < L)
         def _():
             pl.semaphore_wait(ready_z.at[t - 1], 1)
+
+        @pl.when((pos + 1 < L) if t == 1 else (pos == 0))
+        def _():
             for u in range(PARTS):
                 cot_copy(at, u, z_recv.at[L - t - 1, u], at + 2 * t).start()
 
@@ -306,9 +318,23 @@
 
     def cot_piece(i, u):
         higher = L - 1 - pos
-        d = jnp.where(i < higher, i + 1, L - 1 - (i - higher))
-        k = 2 * lax.rem(pos + d, L) + x
+        source = jnp.where(i < higher, pos + i + 1, pos - 1 - (i - higher))
+        if i > 0:
+            source = jnp.where(pos == 0, L - 1 if i == 1 else i, source)
+            source = jnp.where(pos == L - 1, 0 if i == 1 else L - 1 - i, source)
+        d = lax.rem(source - pos + L, L)
+        k = 2 * source + x
         cot_copy(k, u, z_recv.at[d - 1, u], partner).wait_recv()
+        inner = (source > 0) & (source < L - 1)
+
+        @pl.when(inner & (source > pos) & (pos > 0))
+        def _():
+            cot_copy(k, u, z_recv.at[d, u], at - 2).start()
+
+        @pl.when(inner & (source < pos) & (pos < L - 1))
+        def _():
+            cot_copy(k, u, z_recv.at[d - 2, u], at + 2).start()
+
         cot_copy(k, u, x_recv, partner).start()
 
     def inner_step():
@@ -395,7 +421,7 @@
     pairs = list(zip(refs[:count], refs[count:-1]))
     for i, (source, target) in enumerate(pairs):
         rows = source.shape[-2]
-        cuts = 3 if rows % 48 == 0 else 1
+        cuts = 1
         for n in range(cuts):
             part = pl.ds(n * (rows // cuts), rows // cuts)
             index = (0, part) if len(source.shape) == 3 else (part,)
@@ -442,7 +468,7 @@
             pltpu.VMEM((C, height, EXTRA * (W // H)), bf16),
             pltpu.VMEM((height, EXTRA * (W // H)), f32),
             pltpu.VMEM((2 * C * C * (H + EXTRA), height, W // H), bf16),
-            dma((5 + 2 * C,)),
+            dma((7 + 2 * C,)),
             dma((3,)),
             dma((C, CUTS)),
             dma((2,)),

time: 18.4 us -> 18.3 us (level)
  no operation moved by 1% of the time
where the time goes in v3:
time: 18.3 us; the launch traced here: 18.1 us
  Pallas kernels  17.5 us (96%)
  between operations  0.64 us (3%)
    pallas_call x1, Pallas kernels, local(): pl.pallas_call(functools.partial(kernel, R, S), out_shape=tuple((pltpu.VM...  15.7 us
    pallas_call x1, Pallas kernels, store(): pl.pallas_call(store_kernel, out_shape=tuple((jax.ShapeDtypeStruct(a.shap...  1.77 us

profile of v3, /device:TPU:0, one launch (start us, length us, event | category | flops | bytes accessed | tf_op | source)
XLA Modules:
  0.0 18.1 jit_solution(17204909896696050110)
XLA Ops:
  0.6 15.7 %shard_map.127 = (f32[48,8192]{1,0:T(8,128)S(1)}, bf16[1,48,8192]{2,1,0:T(8,128)(2,1)S(1)}, f32[48,2048]{1,0:T(8,128)S(1)}, f32[1,48,1024]{2,1,0:T(8,128)S(1)}, ...) custom-call(f32[48,8192]{1,0:T(8,128)} %anchor_h.1, bf16[1,48,8192]{2,1,0:T(8,128)(2,1)} %rows_h.1, ...), custom_call_target="tpu_custom_call" | custom-call | tf_op jit(solution)/shard_map/pallas_call | solution.py:455
  16.4 1.8 %shard_map.128 = (f32[48,8192]{1,0:T(8,128)}, bf16[1,48,8192]{2,1,0:T(8,128)(2,1)}, f32[48,2048]{1,0:T(8,128)}, f32[1,48,1024]{2,1,0:T(8,128)}, f32[1,48,1024]{2,1,0:T(8,128)}, /*index=5*/f32[1,48,1024]{2,1,0:T(8,128)}) custom-call(f32[48,8192]{1,0:T(8,128)S(1)} %get-tuple-element.12.refs_0_, bf16[1,48,8192]{2,1,0:T(8,128)(2,1)S(1)} %get-tuple-element.13.refs_1_, ...), custom_call_target="tpu_custom_call" | custom-call | tf_op jit(solution)/shard_map/pallas_call | solution.py:434

commit v4 on v3

--- a/solution.py
+++ b/solution.py
@@ -23,14 +23,12 @@
 PARTS = 4
 CUTS = 2
 EXTRA = 1
-LAG = 3
 
 
 def kernel(R, S, anchor_h, rows_h, vel_h, feat_h, cot_h, w_h, m_h, s_h,
            na_o, mg_o, nv_o, nw_o, nm_o, ns_o,
            anchor, rows, vel, feat, cot, wms, sib_rows, more_rows, more_vel, msg,
-           in_sem, sends, sib_recv, more_recv, y_recv, more_y, own_recv, fwd_recv, high_fwd, more_fwd,
-           z_recv, x_recv, ready_y, ready_x, ready_z):
+           in_sem, sends, sib_recv, more_recv, y_recv, more_y, z_recv, x_recv, ready_y, ready_x, ready_z):
     C, L, H = R // 2, S // 2, SPLIT
     LOW = H - EXTRA
     me, at = lax.axis_index("replica"), lax.axis_index("shard")
@@ -78,8 +76,9 @@
         def _():
             tell(barrier, shard=at + 2 * t)
 
-    FIRST, OUT, COT, VEL, FEAT, WMS, REST, KEEP = range(8)
+    FIRST, OUT, COT, VEL, INNER, REST, KEEP = range(7)
     NEAR = KEEP + C
+    own_recv, high_fwd, more_fwd = in_sem.at[FIRST], in_sem.at[VEL], in_sem.at[COT]
 
     def load(src, dst, slot):
         copy = pltpu.make_async_copy(src, dst, in_sem.at[slot])
@@ -160,9 +159,9 @@
                 sib_copy(turn(r), g).start()
     for q in [2 * turn(0) + c] + [2 * turn(r) + 1 - c for r in range(C)]:
         load(anchor_h.at[:, quarter(q)], anchor.at[:, quarter(q)], REST)
-    load(feat_h.at[0], feat, FEAT)
+    load(feat_h.at[0], feat, INNER)
     for n, source in enumerate((w_h, m_h, s_h)):
-        load(source.at[0], wms.at[n], WMS)
+        load(source.at[0], wms.at[n], INNER)
     cot_load.wait()
     pl.when(c == 0)(left_sends)
 
@@ -181,6 +180,10 @@
     def to_sib(t, p, j, h, recv):
         src = lax.rem(y + C - t, C)
         return remote(message(p, src, j, h), message(p, src, j, h), 1, recv, replica=sib)
+
+    def more_across(t, j, n):
+        block = message(0, y, j, LOW + n)
+        return remote(block, block, 1, more_y.at[t - 1, C - 1, n], replica=2 * lax.rem(y + t, C))
 
     def add_message(p, r, h, other_rows, velocity):
         j = turn(r)
@@ -254,6 +257,8 @@
                 h, inner = LOW + n, pl.ds(n * piece, piece)
                 add_message(0, r, h, more_rows[turn(r), :, inner], more_vel[:, inner])
                 for t in range(1, C):
+                    if r == C - 1:
+                        more_across(t, turn(r), n).start()
                     y_copy(t, 0, turn(r), h, more_y.at[t - 1, r, n]).start()
                 own_to_sib(0, turn(r), h).start()
 
@@ -305,14 +310,22 @@
     def more_piece(r, n):
         for t in range(1, C):
             y_copy(t, 0, came(r), LOW + n, more_y.at[t - 1, sent(r, t), n]).wait_recv()
-            to_sib(t, 0, came(r), LOW + n, more_fwd).start()
+            if sent(r, t) < C - 1:
+                to_sib(t, 0, came(r), LOW + n, more_fwd).start()
         finish(0, came(r), LOW + n)
+
+    def more_own(r, n):
+        for t in range(1, C):
+            if sent(r, t) == C - 1:
+                more_across(t, came(r), n).wait_recv()
+        finish(0, came(r), LOW + n)
+        finish_velocity(r, LOW + n)
 
     def pieces_from_sib(n, semaphore):
         whole(msg.at[:n], semaphore).wait_recv()
 
     def low_group(r):
-        pieces_from_sib((C - 1) * LOW, fwd_recv.at[r])
+        pieces_from_sib((C - 1) * LOW, in_sem.at[KEEP + r])
         for h in range(LOW):
             finish(1 - c, came(r), h)
 
@@ -339,8 +352,8 @@
 
     def inner_step():
         whole(cot.at[:L * depth], x_recv).wait_recv()
-        pltpu.make_async_copy(feat_h.at[0], feat, in_sem.at[FEAT]).wait()
-        pltpu.make_async_copy(wms, wms, in_sem.at[WMS]).wait()
+        cols = pl.ds(0, 3 * wms.shape[2] + feat.shape[1] // 2)
+        pltpu.make_async_copy(anchor_h.at[:, cols], anchor.at[:, cols], in_sem.at[INNER]).wait()
         tile = min(256, nw_o.shape[2])
         for n in range(nw_o.shape[2] // tile):
             part = slice(n * tile, (n + 1) * tile)
@@ -360,8 +373,7 @@
     for i, (r, h) in enumerate(low):
         for step in todo[i * each:(i + 1) * each]:
             cot_piece(*step)
-        own_piece(r, h, fwd_recv.at[r])
-        if i == LAG - 1:
+        if i == 0:
             @pl.when(c == 0)
             def _():
                 pieces_from_sib(C * (H + EXTRA), own_recv)
@@ -370,6 +382,7 @@
             def _():
                 pieces_from_sib(C * LOW, own_recv)
 
+        own_piece(r, h, in_sem.at[KEEP + r])
         if h == LOW - 1:
             ready.append(r)
         if len(ready) > 1 and h == LOW - 2:
@@ -382,10 +395,12 @@
                 own_piece(r, h, high_fwd)
         for r in ready:
             low_group(r)
-        for r in range(C):
+        for r in range(C - 1):
             for n in range(EXTRA):
                 more_piece(r, n)
         inner_step()
+        for n in range(EXTRA):
+            more_piece(C - 1, n)
 
     @pl.when(c == 0)
     def _():
@@ -396,11 +411,10 @@
             for h in range(LOW, H):
                 finish(1, came(r), h)
         inner_step()
-        pieces_from_sib((C - 1) * C * EXTRA, more_fwd)
+        pieces_from_sib((C - 1) * (C - 1) * EXTRA, more_fwd)
         for r in range(C):
-            for h in range(LOW, H):
-                finish(0, came(r), h)
-                finish_velocity(r, h)
+            for n in range(EXTRA):
+                more_own(r, n)
 
     whole(cot.at[:(2 * L - 1) * depth], sends.at[2]).wait_send()
 
@@ -468,16 +482,12 @@
             pltpu.VMEM((C, height, EXTRA * (W // H)), bf16),
             pltpu.VMEM((height, EXTRA * (W // H)), f32),
             pltpu.VMEM((2 * C * C * (H + EXTRA), height, W // H), bf16),
-            dma((7 + 2 * C,)),
+            dma((6 + 2 * C,)),
             dma((3,)),
             dma((C, CUTS)),
             dma((2,)),
             dma((C - 1, C, H)),
             dma((C - 1, C, EXTRA)),
-            dma,
-            dma((C,)),
-            dma,
-            dma,
             dma((max(L - 1, 1), PARTS)),
             dma,
             regular,

time: 18.3 us -> 17.9 us (0.978)
  Pallas kernels: 17.5 us -> 17.1 us
    pallas_call x1, Pallas kernels: 15.7 us -> 15.3 us  [local(): pl.pallas_call(functools.partial(kernel, R, S), out_shape=tuple((pltpu.VM...]
where the time goes in v4:
time: 17.9 us; the launch traced here: 17.7 us
  Pallas kernels  17.1 us (96%)
  between operations  0.64 us (4%)
    pallas_call x1, Pallas kernels, local(): pl.pallas_call(functools.partial(kernel, R, S), out_shape=tuple((pltpu.VM...  15.3 us
    pallas_call x1, Pallas kernels, store(): pl.pallas_call(store_kernel, out_shape=tuple((jax.ShapeDtypeStruct(a.shap...  1.77 us

profile of v4, /device:TPU:0, one launch (start us, length us, event | category | flops | bytes accessed | tf_op | source)
XLA Modules:
  0.0 17.7 jit_solution(11059192539277854815)
XLA Ops:
  0.6 15.3 %shard_map.127 = (f32[48,8192]{1,0:T(8,128)S(1)}, bf16[1,48,8192]{2,1,0:T(8,128)(2,1)S(1)}, f32[48,2048]{1,0:T(8,128)S(1)}, f32[1,48,1024]{2,1,0:T(8,128)S(1)}, ...) custom-call(f32[48,8192]{1,0:T(8,128)} %anchor_h.1, bf16[1,48,8192]{2,1,0:T(8,128)(2,1)} %rows_h.1, ...), custom_call_target="tpu_custom_call" | custom-call | tf_op jit(solution)/shard_map/pallas_call | solution.py:469
  16.0 1.8 %shard_map.128 = (f32[48,8192]{1,0:T(8,128)}, bf16[1,48,8192]{2,1,0:T(8,128)(2,1)}, f32[48,2048]{1,0:T(8,128)}, f32[1,48,1024]{2,1,0:T(8,128)}, f32[1,48,1024]{2,1,0:T(8,128)}, /*index=5*/f32[1,48,1024]{2,1,0:T(8,128)}) custom-call(f32[48,8192]{1,0:T(8,128)S(1)} %get-tuple-element.12.refs_0_, bf16[1,48,8192]{2,1,0:T(8,128)(2,1)S(1)} %get-tuple-element.13.refs_1_, ...), custom_call_target="tpu_custom_call" | custom-call | tf_op jit(solution)/shard_map/pallas_call | solution.py:448

commit v5 on v4

--- a/solution.py
+++ b/solution.py
@@ -60,6 +60,18 @@
     def tell(semaphore, **target):
         pl.semaphore_signal(semaphore, inc=1, device_id=target, device_id_type=MESH)
 
+    FIRST, COT, INNER, REST, KEEP, OUT = range(6)
+    NEAR = OUT + 1
+    own_recv, high_fwd, more_fwd = in_sem.at[FIRST], in_sem.at[KEEP], in_sem.at[COT]
+
+    def load(src, dst, slot):
+        copy = pltpu.make_async_copy(src, dst, in_sem.at[slot])
+        copy.start()
+        return copy
+
+    first_cols = columns(2 * turn(0) + 1 - c, 0, per)
+    load(rows_h.at[0, :, first_cols], rows.at[:, first_cols], FIRST)
+
     barrier = pltpu.get_barrier_semaphore()
     tell(barrier, replica=sib)
     for t in range(1, C):
@@ -76,26 +88,18 @@
         def _():
             tell(barrier, shard=at + 2 * t)
 
-    FIRST, OUT, COT, VEL, INNER, REST, KEEP = range(7)
-    NEAR = KEEP + C
-    own_recv, high_fwd, more_fwd = in_sem.at[FIRST], in_sem.at[VEL], in_sem.at[COT]
-
-    def load(src, dst, slot):
-        copy = pltpu.make_async_copy(src, dst, in_sem.at[slot])
-        copy.start()
-        return copy
-
     for r in range(C):
         for g in range(CUTS):
-            cols = columns(2 * turn(r) + 1 - c, g * per, per)
-            load(rows_h.at[0, :, cols], rows.at[:, cols], OUT if r or g else FIRST)
+            if r or g:
+                cols = columns(2 * turn(r) + 1 - c, g * per, per)
+                load(rows_h.at[0, :, cols], rows.at[:, cols], OUT)
     cot_load = load(cot_h.at[0], cot.at[tokens(at)], COT)
-    keep_load, near_load = [], []
+    near_load = []
     for r in range(C):
         cols = quarter(2 * turn(r) + c)
-        keep_load.append(load(rows_h.at[0, :, cols], rows.at[:, cols], KEEP + r))
+        load(rows_h.at[0, :, cols], rows.at[:, cols], KEEP)
         if r == 0:
-            vel_load = load(vel_h, vel, VEL)
+            load(vel_h, vel, KEEP)
         else:
             near_load.append(load(anchor_h.at[:, cols], anchor.at[:, cols], NEAR + r - 1))
 
@@ -112,7 +116,7 @@
     for t in range(1, L):
         @pl.when(pos >= t)
         def _():
-            tell(ready_z.at[t - 1], shard=at - 2 * t)
+            tell(ready_z.at[min(t, 2) - 1], shard=at - 2 * t)
 
     def remote(src, dst, send, recv, **target):
         return pltpu.make_async_remote_copy(
@@ -130,10 +134,10 @@
 
     def more_copy(j):
         cols = columns(2 * j, LOW, EXTRA)
-        return remote(rows.at[:, cols], more_rows.at[j], 0, more_recv.at[0], replica=sib)
+        return remote(rows.at[:, cols], more_rows.at[j], 0, more_recv, replica=sib)
 
     def more_vel_copy():
-        return remote(vel.at[:, pl.ds(LOW * piece, EXTRA * piece)], more_vel, 0, more_recv.at[1], replica=sib)
+        return remote(vel.at[:, pl.ds(LOW * piece, EXTRA * piece)], more_vel, 0, more_recv, replica=sib)
 
     def cot_copy(k, u, recv, target):
         block = cot.at[tokens(k), pl.ds(u * part_width, part_width)]
@@ -163,7 +167,7 @@
     for n, source in enumerate((w_h, m_h, s_h)):
         load(source.at[0], wms.at[n], INNER)
     cot_load.wait()
-    pl.when(c == 0)(left_sends)
+    pl.when((c == 0) | (pos < L - 1))(left_sends)
 
     def slot(p, src, j, h):
         return ((p * C + src) * C + j) * H + h
@@ -198,17 +202,16 @@
     def from_sib(j, h):
         return sib_rows[j, h // per, :, pl.ds(h % per * piece, piece)]
 
+    halves = pl.ds(0, C * W // 2 + W)
+    pltpu.make_async_copy(anchor_h.at[:, halves], anchor.at[:, halves], in_sem.at[KEEP]).wait()
     for r in range(C):
         j = turn(r)
-        keep_load[r].wait()
 
         @pl.when(c == 0)
         def _():
             more_copy(j).start()
 
         if r == 0:
-            vel_load.wait()
-
             @pl.when(c == 0)
             def _():
                 more_vel_copy().start()
@@ -236,7 +239,7 @@
                 pl.when(c == 1)(handle)
 
         if r == 0:
-            pl.when(c == 1)(left_sends)
+            pl.when((c == 1) & (pos == L - 1))(left_sends)
 
     @pl.when(x == 0)
     def _():
@@ -250,8 +253,7 @@
 
     @pl.when(c == 1)
     def _():
-        whole(more_rows, more_recv.at[0]).wait_recv()
-        more_vel_copy().wait_recv()
+        whole(rows.at[:, pl.ds(0, (C + 2) * EXTRA * piece)], more_recv).wait_recv()
         for r in range(C):
             for n in range(EXTRA):
                 h, inner = LOW + n, pl.ds(n * piece, piece)
@@ -262,13 +264,19 @@
                     y_copy(t, 0, turn(r), h, more_y.at[t - 1, r, n]).start()
                 own_to_sib(0, turn(r), h).start()
 
-    for t in range(1, L):
-        @pl.when(pos + t < L)
-        def _():
-            pl.semaphore_wait(ready_z.at[t - 1], 1)
-
-        @pl.when((pos + 1 < L) if t == 1 else (pos == 0))
-        def _():
+    @pl.when(pos + 1 < L)
+    def _():
+        pl.semaphore_wait(ready_z.at[0], 1)
+        for u in range(PARTS):
+            cot_copy(at, u, z_recv.at[L - 2, u], at + 2).start()
+
+    @pl.when(pos + 2 < L)
+    def _():
+        pl.semaphore_wait(ready_z.at[1], L - 2 - pos)
+
+    @pl.when(pos == 0)
+    def _():
+        for t in range(2, L):
             for u in range(PARTS):
                 cot_copy(at, u, z_recv.at[L - t - 1, u], at + 2 * t).start()
 
@@ -325,13 +333,14 @@
         whole(msg.at[:n], semaphore).wait_recv()
 
     def low_group(r):
-        pieces_from_sib((C - 1) * LOW, in_sem.at[KEEP + r])
+        pieces_from_sib((C - 1) * LOW, in_sem.at[OUT + r])
         for h in range(LOW):
             finish(1 - c, came(r), h)
 
     def cot_piece(i, u):
         higher = L - 1 - pos
         source = jnp.where(i < higher, pos + i + 1, pos - 1 - (i - higher))
+        source = jnp.where(pos == L - 2, pos - 1 - i if i < L - 2 else L - 1, source)
         if i > 0:
             source = jnp.where(pos == 0, L - 1 if i == 1 else i, source)
             source = jnp.where(pos == L - 1, 0 if i == 1 else L - 1 - i, source)
@@ -382,7 +391,7 @@
             def _():
                 pieces_from_sib(C * LOW, own_recv)
 
-        own_piece(r, h, in_sem.at[KEEP + r])
+        own_piece(r, h, in_sem.at[OUT + r])
         if h == LOW - 1:
             ready.append(r)
         if len(ready) > 1 and h == LOW - 2:
@@ -406,11 +415,11 @@
     def _():
         for r in ready:
             low_group(r)
+        inner_step()
         pieces_from_sib((C - 1) * C * EXTRA, high_fwd)
         for r in range(C):
             for h in range(LOW, H):
                 finish(1, came(r), h)
-        inner_step()
         pieces_from_sib((C - 1) * (C - 1) * EXTRA, more_fwd)
         for r in range(C):
             for n in range(EXTRA):
@@ -482,17 +491,17 @@
             pltpu.VMEM((C, height, EXTRA * (W // H)), bf16),
             pltpu.VMEM((height, EXTRA * (W // H)), f32),
             pltpu.VMEM((2 * C * C * (H + EXTRA), height, W // H), bf16),
-            dma((6 + 2 * C,)),
+            dma((5 + C,)),
             dma((3,)),
             dma((C, CUTS)),
-            dma((2,)),
+            dma,
             dma((C - 1, C, H)),
             dma((C - 1, C, EXTRA)),
             dma((max(L - 1, 1), PARTS)),
             dma,
             regular,
             regular,
-            regular((max(L - 1, 1),)),
+            regular((2,)),
         ],
         compiler_params=pltpu.CompilerParams(
             collective_id=0, has_side_effects=True, vmem_limit_bytes=room),

time: 17.9 us -> 17.7 us (0.989)
  Pallas kernels: 17.1 us -> 16.9 us
where the time goes in v5:
time: 17.7 us; the launch traced here: 17.6 us
  Pallas kernels  16.9 us (95%)
  between operations  0.64 us (4%)
    pallas_call x1, Pallas kernels, local(): pl.pallas_call(functools.partial(kernel, R, S), out_shape=tuple((pltpu.VM...  15.2 us
    pallas_call x1, Pallas kernels, store(): pl.pallas_call(store_kernel, out_shape=tuple((jax.ShapeDtypeStruct(a.shap...  1.77 us

profile of v5, /device:TPU:0, one launch (start us, length us, event | category | flops | bytes accessed | tf_op | source)
XLA Modules:
  0.0 17.6 jit_solution(16042233855693280333)
XLA Ops:
  0.6 15.2 %shard_map.127 = (f32[48,8192]{1,0:T(8,128)S(1)}, bf16[1,48,8192]{2,1,0:T(8,128)(2,1)S(1)}, f32[48,2048]{1,0:T(8,128)S(1)}, f32[1,48,1024]{2,1,0:T(8,128)S(1)}, ...) custom-call(f32[48,8192]{1,0:T(8,128)} %anchor_h.1, bf16[1,48,8192]{2,1,0:T(8,128)(2,1)} %rows_h.1, ...), custom_call_target="tpu_custom_call" | custom-call | tf_op jit(solution)/shard_map/pallas_call | solution.py:478
  15.8 1.8 %shard_map.128 = (f32[48,8192]{1,0:T(8,128)}, bf16[1,48,8192]{2,1,0:T(8,128)(2,1)}, f32[48,2048]{1,0:T(8,128)}, f32[1,48,1024]{2,1,0:T(8,128)}, f32[1,48,1024]{2,1,0:T(8,128)}, /*index=5*/f32[1,48,1024]{2,1,0:T(8,128)}) custom-call(f32[48,8192]{1,0:T(8,128)S(1)} %get-tuple-element.12.refs_0_, bf16[1,48,8192]{2,1,0:T(8,128)(2,1)S(1)} %get-tuple-element.13.refs_1_, ...), custom_call_target="tpu_custom_call" | custom-call | tf_op jit(solution)/shard_map/pallas_call | solution.py:457

commit v6 on v5

--- a/solution.py
+++ b/solution.py
@@ -27,8 +27,8 @@
 
 def kernel(R, S, anchor_h, rows_h, vel_h, feat_h, cot_h, w_h, m_h, s_h,
            na_o, mg_o, nv_o, nw_o, nm_o, ns_o,
-           anchor, rows, vel, feat, cot, wms, sib_rows, more_rows, more_vel, msg,
-           in_sem, sends, sib_recv, more_recv, y_recv, more_y, z_recv, x_recv, ready_y, ready_x, ready_z):
+           anchor, rows, vel, feat, cot, wms, sib_rows, more_rows, more_vel, msg, passing,
+           in_sem, sends, sib_recv, more_recv, y_recv, more_y, pass_recv, z_recv, x_recv, ready_y, ready_x, ready_z):
     C, L, H = R // 2, S // 2, SPLIT
     LOW = H - EXTRA
     me, at = lax.axis_index("replica"), lax.axis_index("shard")
@@ -199,6 +199,16 @@
             value = 2.0 * anchor[:, cols] - both
         msg[slot(p, y, j, h)] = value.astype(jnp.bfloat16)
 
+    goes_around = (y == 1) & (x == 0)
+    passes_on = (c == 1) & (y == 0) & (x == 1)
+
+    def around(r, h):
+        return C == 2 and r == 0 and h == H - 1
+
+    def pass_copy():
+        return remote(passing, message(1, 1, 1, H - 1), 3,
+                      y_recv.at[0, 0, H - 1], shard=partner)
+
     def from_sib(j, h):
         return sib_rows[j, h // per, :, pl.ds(h % per * piece, piece)]
 
@@ -230,7 +240,24 @@
                         pl.semaphore_wait(ready_y, C - 1 - y)
 
                 for t in range(1, C):
-                    y_copy(t, c, j, h, y_recv.at[t - 1, r, h]).start()
+                    if not around(r, h):
+                        y_copy(t, c, j, h, y_recv.at[t - 1, r, h]).start()
+                if around(r, h):
+                    @pl.when((c == 1) & (x == 0))
+                    def _():
+                        pl.semaphore_wait(ready_x, 1)
+
+                    @pl.when(goes_around)
+                    def _():
+                        block = message(1, y, j, h)
+                        pltpu.make_async_remote_copy(
+                            src_ref=block, dst_ref=passing, send_sem=sends.at[1], recv_sem=pass_recv,
+                            device_id=(me - 2, partner), device_id_type=MESH).start()
+
+                    @pl.when(jnp.logical_not(goes_around))
+                    def _():
+                        y_copy(1, c, j, h, y_recv.at[0, r, h]).start()
+
                 own_to_sib(c, j, h).start()
 
             if h < LOW:
@@ -238,13 +265,11 @@
             else:
                 pl.when(c == 1)(handle)
 
-        if r == 0:
-            pl.when((c == 1) & (pos == L - 1))(left_sends)
-
-    @pl.when(x == 0)
+    @pl.when((x == 0) if C != 2 else (c == 0) & (x == 0))
     def _():
         pl.semaphore_wait(ready_x, 1)
 
+    pl.when((c == 1) & (pos == L - 1))(left_sends)
     for u in range(PARTS):
         cot_copy(at, u, x_recv, partner).start()
 
@@ -392,6 +417,12 @@
                 pieces_from_sib(C * LOW, own_recv)
 
         own_piece(r, h, in_sem.at[OUT + r])
+        if C == 2 and i == 0:
+            @pl.when(passes_on)
+            def _():
+                whole(passing, pass_recv).wait_recv()
+                pass_copy().start()
+
         if h == LOW - 1:
             ready.append(r)
         if len(ready) > 1 and h == LOW - 2:
@@ -402,11 +433,11 @@
         for r in range(C):
             for h in range(LOW, H):
                 own_piece(r, h, high_fwd)
-        for r in ready:
-            low_group(r)
         for r in range(C - 1):
             for n in range(EXTRA):
                 more_piece(r, n)
+        for r in ready:
+            low_group(r)
         inner_step()
         for n in range(EXTRA):
             more_piece(C - 1, n)
@@ -426,6 +457,11 @@
                 more_own(r, n)
 
     whole(cot.at[:(2 * L - 1) * depth], sends.at[2]).wait_send()
+
+    if C == 2:
+        @pl.when(passes_on)
+        def _():
+            pass_copy().wait_send()
 
     @pl.when(c == 0)
     def _():
@@ -491,12 +527,14 @@
             pltpu.VMEM((C, height, EXTRA * (W // H)), bf16),
             pltpu.VMEM((height, EXTRA * (W // H)), f32),
             pltpu.VMEM((2 * C * C * (H + EXTRA), height, W // H), bf16),
+            pltpu.VMEM((height, W // H), bf16),
             dma((5 + C,)),
-            dma((3,)),
+            dma((4,)),
             dma((C, CUTS)),
             dma,
             dma((C - 1, C, H)),
             dma((C - 1, C, EXTRA)),
+            dma,
             dma((max(L - 1, 1), PARTS)),
             dma,
             regular,

time: 17.7 us -> 17.4 us (0.983)
  Pallas kernels: 16.9 us -> 16.6 us
    pallas_call x1, Pallas kernels: 15.2 us -> 14.8 us  [local(): pl.pallas_call(functools.partial(kernel, R, S), out_shape=tuple((pltpu.VM...]
where the time goes in v6:
time: 17.4 us; the launch traced here: 17.3 us
  Pallas kernels  16.6 us (95%)
  between operations  0.64 us (4%)
    pallas_call x1, Pallas kernels, local(): pl.pallas_call(functools.partial(kernel, R, S), out_shape=tuple((pltpu.VM...  14.8 us
    pallas_call x1, Pallas kernels, store(): pl.pallas_call(store_kernel, out_shape=tuple((jax.ShapeDtypeStruct(a.shap...  1.77 us

profile of v6, /device:TPU:0, one launch (start us, length us, event | category | flops | bytes accessed | tf_op | source)
XLA Modules:
  0.0 17.3 jit_solution(15461553943829561137)
XLA Ops:
  0.6 14.8 %shard_map.127 = (f32[48,8192]{1,0:T(8,128)S(1)}, bf16[1,48,8192]{2,1,0:T(8,128)(2,1)S(1)}, f32[48,2048]{1,0:T(8,128)S(1)}, f32[1,48,1024]{2,1,0:T(8,128)S(1)}, ...) custom-call(f32[48,8192]{1,0:T(8,128)} %anchor_h.1, bf16[1,48,8192]{2,1,0:T(8,128)(2,1)} %rows_h.1, ...), custom_call_target="tpu_custom_call" | custom-call | tf_op jit(solution)/shard_map/pallas_call | solution.py:514
  15.5 1.8 %shard_map.128 = (f32[48,8192]{1,0:T(8,128)}, bf16[1,48,8192]{2,1,0:T(8,128)(2,1)}, f32[48,2048]{1,0:T(8,128)}, f32[1,48,1024]{2,1,0:T(8,128)}, f32[1,48,1024]{2,1,0:T(8,128)}, /*index=5*/f32[1,48,1024]{2,1,0:T(8,128)}) custom-call(f32[48,8192]{1,0:T(8,128)S(1)} %get-tuple-element.12.refs_0_, bf16[1,48,8192]{2,1,0:T(8,128)(2,1)S(1)} %get-tuple-element.13.refs_1_, ...), custom_call_target="tpu_custom_call" | custom-call | tf_op jit(solution)/shard_map/pallas_call | solution.py:493

commit v7 on v6

--- a/solution.py
+++ b/solution.py
@@ -206,8 +206,9 @@
         return C == 2 and r == 0 and h == H - 1
 
     def pass_copy():
-        return remote(passing, message(1, 1, 1, H - 1), 3,
-                      y_recv.at[0, 0, H - 1], shard=partner)
+        return pltpu.make_async_remote_copy(
+            src_ref=passing, dst_ref=message(1, 1, 1, H - 1), send_sem=in_sem.at[KEEP],
+            recv_sem=y_recv.at[0, 0, H - 1], device_id={"shard": partner}, device_id_type=MESH)
 
     def from_sib(j, h):
         return sib_rows[j, h // per, :, pl.ds(h % per * piece, piece)]
@@ -388,7 +389,7 @@
         whole(cot.at[:L * depth], x_recv).wait_recv()
         cols = pl.ds(0, 3 * wms.shape[2] + feat.shape[1] // 2)
         pltpu.make_async_copy(anchor_h.at[:, cols], anchor.at[:, cols], in_sem.at[INNER]).wait()
-        tile = min(256, nw_o.shape[2])
+        tile = min(512, nw_o.shape[2])
         for n in range(nw_o.shape[2] // tile):
             part = slice(n * tile, (n + 1) * tile)
             gradient = jnp.dot(feat[...], cot[:, part], preferred_element_type=jnp.float32)
@@ -446,11 +447,11 @@
     def _():
         for r in ready:
             low_group(r)
-        inner_step()
         pieces_from_sib((C - 1) * C * EXTRA, high_fwd)
         for r in range(C):
             for h in range(LOW, H):
                 finish(1, came(r), h)
+        inner_step()
         pieces_from_sib((C - 1) * (C - 1) * EXTRA, more_fwd)
         for r in range(C):
             for n in range(EXTRA):
@@ -529,7 +530,7 @@
             pltpu.VMEM((2 * C * C * (H + EXTRA), height, W // H), bf16),
             pltpu.VMEM((height, W // H), bf16),
             dma((5 + C,)),
-            dma((4,)),
+            dma((3,)),
             dma((C, CUTS)),
             dma,
             dma((C - 1, C, H)),

time: 17.4 us -> 17.4 us (level)
  no operation moved by 1% of the time
where the time goes in v7:
time: 17.4 us; the launch traced here: 17.2 us
  Pallas kernels  16.6 us (95%)
  between operations  0.64 us (4%)
    pallas_call x1, Pallas kernels, local(): pl.pallas_call(functools.partial(kernel, R, S), out_shape=tuple((pltpu.VM...  14.8 us
    pallas_call x1, Pallas kernels, store(): pl.pallas_call(store_kernel, out_shape=tuple((jax.ShapeDtypeStruct(a.shap...  1.77 us

profile of v7, /device:TPU:0, one launch (start us, length us, event | category | flops | bytes accessed | tf_op | source)
XLA Modules:
  0.0 17.2 jit_solution(14773413523381586889)
XLA Ops:
  0.6 14.8 %shard_map.127 = (f32[48,8192]{1,0:T(8,128)S(1)}, bf16[1,48,8192]{2,1,0:T(8,128)(2,1)S(1)}, f32[48,2048]{1,0:T(8,128)S(1)}, f32[1,48,1024]{2,1,0:T(8,128)S(1)}, ...) custom-call(f32[48,8192]{1,0:T(8,128)} %anchor_h.1, bf16[1,48,8192]{2,1,0:T(8,128)(2,1)} %rows_h.1, ...), custom_call_target="tpu_custom_call" | custom-call | tf_op jit(solution)/shard_map/pallas_call | solution.py:515
  15.5 1.8 %shard_map.128 = (f32[48,8192]{1,0:T(8,128)}, bf16[1,48,8192]{2,1,0:T(8,128)(2,1)}, f32[48,2048]{1,0:T(8,128)}, f32[1,48,1024]{2,1,0:T(8,128)}, f32[1,48,1024]{2,1,0:T(8,128)}, /*index=5*/f32[1,48,1024]{2,1,0:T(8,128)}) custom-call(f32[48,8192]{1,0:T(8,128)S(1)} %get-tuple-element.12.refs_0_, bf16[1,48,8192]{2,1,0:T(8,128)(2,1)S(1)} %get-tuple-element.13.refs_1_, ...), custom_call_target="tpu_custom_call" | custom-call | tf_op jit(solution)/shard_map/pallas_call | solution.py:494

commit v8 on v7

--- a/solution.py
+++ b/solution.py
@@ -21,7 +21,7 @@
 MESH = pl.DeviceIdType.MESH
 SPLIT = 4
 PARTS = 4
-CUTS = 2
+CUTS = 4
 EXTRA = 1
 
 

time: 17.4 us -> 17.3 us (level)
  no operation moved by 1% of the time
where the time goes in v8:
time: 17.3 us; the launch traced here: 17.1 us
  Pallas kernels  16.5 us (95%)
  between operations  0.64 us (4%)
    pallas_call x1, Pallas kernels, local(): pl.pallas_call(functools.partial(kernel, R, S), out_shape=tuple((pltpu.VM...  14.7 us
    pallas_call x1, Pallas kernels, store(): pl.pallas_call(store_kernel, out_shape=tuple((jax.ShapeDtypeStruct(a.shap...  1.77 us

profile of v8, /device:TPU:0, one launch (start us, length us, event | category | flops | bytes accessed | tf_op | source)
XLA Modules:
  0.0 17.1 jit_solution(4278427697430097258)
XLA Ops:
  0.6 14.7 %shard_map.127 = (f32[48,8192]{1,0:T(8,128)S(1)}, bf16[1,48,8192]{2,1,0:T(8,128)(2,1)S(1)}, f32[48,2048]{1,0:T(8,128)S(1)}, f32[1,48,1024]{2,1,0:T(8,128)S(1)}, ...) custom-call(f32[48,8192]{1,0:T(8,128)} %anchor_h.1, bf16[1,48,8192]{2,1,0:T(8,128)(2,1)} %rows_h.1, ...), custom_call_target="tpu_custom_call" | custom-call | tf_op jit(solution)/shard_map/pallas_call | solution.py:515
  15.4 1.8 %shard_map.128 = (f32[48,8192]{1,0:T(8,128)}, bf16[1,48,8192]{2,1,0:T(8,128)(2,1)}, f32[48,2048]{1,0:T(8,128)}, f32[1,48,1024]{2,1,0:T(8,128)}, f32[1,48,1024]{2,1,0:T(8,128)}, /*index=5*/f32[1,48,1024]{2,1,0:T(8,128)}) custom-call(f32[48,8192]{1,0:T(8,128)S(1)} %get-tuple-element.12.refs_0_, bf16[1,48,8192]{2,1,0:T(8,128)(2,1)S(1)} %get-tuple-element.13.refs_1_, ...), custom_call_target="tpu_custom_call" | custom-call | tf_op jit(solution)/shard_map/pallas_call | solution.py:494
